TPU v7x, 32 devices: a whole 2x2x4 slice. The times are simulated.
32 devices in a mesh: gx: 4 (over z), gy: 2 (over x), gz: 4 (over y, core).
Axes of the slice: x: 2, y: 2, z: 4, core: 2. Of those that a mesh axis runs over, the one named last changes fastest.
Arguments:
- right_side: float32 [4, 2, 8, 128], P('gx', 'gy', 'gz'), may hold values from -8 to 8
- diag_blocks: float32 [4, 2, 8, 128, 128], P('gx', 'gy', 'gz'), may hold values from -0.035 to 2.04, as said below
- couplings: float32 [3, 4, 2, 8, 128, 128], P(None, 'gx', 'gy', 'gz'), may hold values from -0.04 to 0.04
- pattern: int32 [3, 4, 2, 8], P(None, 'gx', 'gy', 'gz'), may hold values 0 or 1
- deflation: float32 [4, 2, 8, 32, 128], P('gx', 'gy', 'gz'), may hold values from -5 to 5
Outputs:
- solution: float32 [4, 2, 8, 128], P('gx', 'gy', 'gz')
- residual: float32 [4, 2, 8, 128], P('gx', 'gy', 'gz')
Inputs may be any that keep to these rules, and one draw needn't show every extreme that they name: `diag_blocks`: each diagonal block is symmetric.
All inputs are finite; a program needn't handle non-finite values. No bound on the sum of `pattern` on one device may be relied on, other than what follows from the above.
Results may differ from a plain program's by a relative error of at most 0.00035.
Values sent between devices are 32-bit elements; how exact they have to be, the bound alone decides.
A program may use at most 64 MiB of HBM per device.

v0:
```python
import jax
import jax.numpy as jnp
from jax import lax
from jax.sharding import PartitionSpec as P

ITERS = 3


HIGHEST = lax.Precision.HIGHEST


def shifted(block, axis, distance):
    devices = range(lax.axis_size(axis))
    route = [(i - distance, i) for i in devices if i - distance in devices]
    return lax.ppermute(block, axis, route)


def rows_times(blocks, vectors):
    return jnp.einsum("xyzrk,xyzck->xyzcr", blocks, vectors, precision=HIGHEST)


def cols_times(blocks, vectors):
    return jnp.einsum("xyzkr,xyzck->xyzcr", blocks, vectors, precision=HIGHEST)


def spread(coarse_coef, basis):
    return jnp.einsum("a,xyzak->xyzk", coarse_coef, basis, precision=HIGHEST)


def pushed_product(diag_blocks, couplings, weights, vectors):
    accum_sum = rows_times(diag_blocks, vectors)
    gate_x = weights[0][:, :, :, None, None]
    beyond = shifted(vectors, "gx", -1)
    accum_sum = accum_sum + gate_x * rows_times(
        couplings[0], jnp.concatenate([vectors[1:], beyond], axis=0)
    )
    carried = gate_x * cols_times(couplings[0], vectors)
    arrived = shifted(carried, "gx", 1)
    accum_sum = accum_sum + jnp.concatenate([arrived, carried[:-1]], axis=0)
    gate_y = weights[1][:, :, :, None, None]
    beyond = shifted(vectors, "gy", -1)
    accum_sum = accum_sum + gate_y * rows_times(
        couplings[1], jnp.concatenate([vectors[:, 1:], beyond], axis=1)
    )
    carried = gate_y * cols_times(couplings[1], vectors)
    arrived = shifted(carried, "gy", 1)
    accum_sum = accum_sum + jnp.concatenate([arrived, carried[:, :-1]], axis=1)
    gate_z = weights[2][:, :, :, None, None]
    beyond = shifted(vectors[:, :, :1], "gz", -1)
    accum_sum = accum_sum + gate_z * rows_times(
        couplings[2], jnp.concatenate([vectors[:, :, 1:], beyond], axis=2)
    )
    carried = gate_z * cols_times(couplings[2], vectors)
    arrived = shifted(carried[:, :, -1:], "gz", 1)
    accum_sum = accum_sum + jnp.concatenate([arrived, carried[:, :, :-1]], axis=2)
    return accum_sum


def joint_of(residual, image_res, applied):
    local_sq = jnp.sum(residual * residual)
    local_cross = jnp.sum(residual * image_res)
    local_proj = jnp.einsum("xyzak,xyzk->a", applied, residual, precision=HIGHEST)
    return lax.psum((local_sq, local_cross, local_proj), ("gx", "gy", "gz"))


def per_device(right_side, diag_blocks, couplings, pattern, deflation):
    weights = pattern.astype(jnp.float32)

    def operate(vectors):
        return pushed_product(diag_blocks, couplings, weights, vectors)

    applied = operate(deflation)
    local_coarse = jnp.einsum("xyzak,xyzbk->ab", deflation, applied, precision=HIGHEST)
    local_right = jnp.einsum("xyzak,xyzk->a", deflation, right_side, precision=HIGHEST)
    coarse_mat, projected = lax.psum((local_coarse, local_right), ("gx", "gy", "gz"))
    coarse_mat = 0.5 * (coarse_mat + coarse_mat.T)
    factor = jnp.linalg.cholesky(coarse_mat)
    coarse_coef = jax.scipy.linalg.cho_solve((factor, True), projected)
    solution = spread(coarse_coef, deflation)
    residual = right_side - spread(coarse_coef, applied)

    def apply_vector(vectors):
        return operate(vectors[:, :, :, None, :])[:, :, :, 0, :]

    image_res = apply_vector(residual)
    norm_sq, cross_val, projected = joint_of(residual, image_res, applied)
    coarse_coef = jax.scipy.linalg.cho_solve((factor, True), projected)
    direction = residual - spread(coarse_coef, deflation)
    images = image_res - spread(coarse_coef, applied)
    curv_val = cross_val - jnp.dot(projected, coarse_coef)
    for iteration in range(ITERS):
        step_len = norm_sq / curv_val
        solution = solution + step_len * direction
        residual = residual - step_len * images
        if iteration + 1 < ITERS:
            image_res = apply_vector(residual)
            norm_new, cross_val, projected = joint_of(residual, image_res, applied)
            coarse_coef = jax.scipy.linalg.cho_solve((factor, True), projected)
            growth = norm_new / norm_sq
            direction = residual + growth * direction - spread(coarse_coef, deflation)
            images = image_res + growth * images - spread(coarse_coef, applied)
            curv_val = cross_val - growth * growth * curv_val - jnp.dot(projected, coarse_coef)
            norm_sq = norm_new
    return (solution, residual)


def solution(mesh):
    in_specs = (
        P("gx", "gy", "gz", None),
        P("gx", "gy", "gz", None, None),
        P(None, "gx", "gy", "gz", None, None),
        P(None, "gx", "gy", "gz"),
        P("gx", "gy", "gz", None, None),
    )
    out_specs = (P("gx", "gy", "gz", None), P("gx", "gy", "gz", None))
    return jax.shard_map(
        per_device, mesh=mesh, in_specs=in_specs, out_specs=out_specs, check_vma=False
    )
```

profile of v0, /device:TPU:0, one launch (start us, length us, event | category | flops | bytes accessed | tf_op | source)
XLA Modules:
  0.0 266.5 jit_solution(15322092795217254668)
XLA Ops:
  0.7 1.4 collective-permute-start.2
  2.1 1.3 collective-permute-start
  3.4 0.7 fusion.147
  4.1 1.3 collective-permute-start.4
  5.4 0.7 convert_element_type.3
  6.3 1.1 fusion
  7.4 3.0 %collective-permute-start.5 = (f32[1,1,1,32,128]{4,3,2,1,0:T(8,128)S(1)}, f32[1,1,1,32,128]{4,3,2,1,0:T(8,128)S(1)}, u32[]{:S(2)}, u32[]{:S(2)}) collective-permute-start(f32[1,1,1,32,128]{4,3,2,1,0:T(8,128)S(1)} %get-tuple-element.28), channel_id=1, source_target_pairs={{0,1},{1,2},{2,3},{4,5},{5,6},{6,7},{8,9},{9,10},{10,11},{12,13},{... | collective-permute-start | bytes 49160 | tf_op jit(solution)/shard_map/ppermute | solution.py:15
  10.5 1.1 fusion.4
  11.6 5.6 %collective-permute-start.1 = (f32[1,1,2,32,128]{4,3,2,1,0:T(8,128)S(1)}, f32[1,1,2,32,128]{4,3,2,1,0:T(8,128)S(1)}, u32[]{:S(2)}, u32[]{:S(2)}) collective-permute-start(f32[1,1,2,32,128]{4,3,2,1,0:T(8,128)S(1)} %fusion.4), channel_id=1, source_target_pairs={{0,8},{8,16},{16,24},{1,9},{9,17},{17,25},{2,10},{10,18},{18,26},{... | collective-permute-start | bytes 98312 | tf_op jit(solution)/shard_map/ppermute | solution.py:15
  17.8 0.7 copy-done.3
  18.6 4.5 %collective-permute-start.3 = (f32[1,1,2,32,128]{4,3,2,1,0:T(8,128)S(1)}, f32[1,1,2,32,128]{4,3,2,1,0:T(8,128)S(1)}, u32[]{:S(2)}, u32[]{:S(2)}) collective-permute-start(f32[1,1,2,32,128]{4,3,2,1,0:T(8,128)S(1)} %fusion.2), channel_id=1, source_target_pairs={{0,4},{1,5},{2,6},{3,7},{8,12},{9,13},{10,14},{11,15},{16,20},{17,... | collective-permute-start | bytes 98312 | tf_op jit(solution)/shard_map/ppermute | solution.py:15
  23.8 0.9 collective-permute-done.3
  24.8 0.3 fusion.12
  25.3 41.9 %all-reduce.3 = (f32[32,32]{0,1:T(8,128)S(1)}, f32[32]{0:T(128)S(1)}) all-reduce(f32[32,32]{0,1:T(8,128)S(1)} %convolution_bitcast_fusion, f32[32]{0:T(128)S(1)} %convolution_bitcast_fusion.4), channel_id=1, replica_groups=mesh['gx'=4,'gy'=2,'gz'=4] {'gx','gy','gz'}, use_global_device_ids=true, to_apply=%region_0.0 | all-reduce | flops 1056 | bytes 8448 | tf_op jit(solution)/shard_map/psum | solution.py:75
  67.3 2.9 %cholesky.18 = f32[32,32]{1,0:T(8,128)S(1)} custom-call(f32[32,32]{1,0:T(8,128)S(1)} %fusion.117), custom_call_target="Cholesky" | custom-call | tf_op jit(solution)/shard_map/jit(cholesky)/cholesky | solution.py:77
  70.3 0.6 compare_reduce_fusion
  70.9 0.7 fusion.105
  71.6 2.4 custom-call.11
  75.3 1.3 collective-permute-start.6
  76.6 1.3 collective-permute-start.8
  78.3 1.3 collective-permute-start.10
  79.7 4.5 %collective-permute-start.7 = (f32[1,1,2,1,128]{4,2,3,1,0:T(2,128)S(1)}, f32[1,1,2,1,128]{4,2,3,1,0:T(2,128)S(1)}, u32[]{:S(2)}, u32[]{:S(2)}) collective-permute-start(f32[1,1,2,1,128]{4,2,3,1,0:T(2,128)S(1)} %multiply_bitcast_fusion.8), channel_id=1, source_target_pairs={{0,8},{8,16},{16,24},{1,9},{9,17},{17,25},{2,10},{10,18},{18,26},{... | collective-permute-start | bytes 3080 | tf_op jit(solution)/shard_map/ppermute | solution.py:15
  84.3 4.5 %collective-permute-start.9 = (f32[1,1,2,1,128]{4,2,3,1,0:T(2,128)S(1)}, f32[1,1,2,1,128]{4,2,3,1,0:T(2,128)S(1)}, u32[]{:S(2)}, u32[]{:S(2)}) collective-permute-start(f32[1,1,2,1,128]{4,2,3,1,0:T(2,128)S(1)} %multiply_bitcast_fusion.7), channel_id=1, source_target_pairs={{0,4},{1,5},{2,6},{3,7},{8,12},{9,13},{10,14},{11,15},{16,20},{17,... | collective-permute-start | bytes 3080 | tf_op jit(solution)/shard_map/ppermute | solution.py:15
  88.9 2.5 collective-permute-start.11
  91.7 0.3 fusion.51
  92.4 0.7 fusion.126
  93.1 40.6 %all-reduce.2 = (f32[]{:T(128)}, f32[]{:T(128)}, f32[32]{0:T(128)S(1)}) all-reduce(f32[]{:T(128)} %get-tuple-element.8, f32[]{:T(128)} %get-tuple-element.7, f32[32]{0:T(128)S(1)} %convolution_bitcast_fusion.3), channel_id=1, replica_groups=mesh['gx'=4,'gy'=2,'gz'=4] {'gx','gy','gz'}, use_global_device_ids=true, to_apply=%region_5.7 | all-reduce | flops 34 | bytes 272 | tf_op jit(solution)/shard_map/psum | solution.py:63
  133.8 0.8 fusion.141
  137.5 1.3 collective-permute-start.12
  138.8 1.3 collective-permute-start.14
  140.6 1.3 collective-permute-start.16
  142.0 4.5 %collective-permute-start.13 = (f32[1,1,2,1,128]{4,2,3,1,0:T(2,128)S(1)}, f32[1,1,2,1,128]{4,2,3,1,0:T(2,128)S(1)}, u32[]{:S(2)}, u32[]{:S(2)}) collective-permute-start(f32[1,1,2,1,128]{4,2,3,1,0:T(2,128)S(1)} %multiply_bitcast_fusion.5), channel_id=1, source_target_pairs={{0,8},{8,16},{16,24},{1,9},{9,17},{17,25},{2,10},{10,18},{18,26},{... | collective-permute-start | bytes 3080 | tf_op jit(solution)/shard_map/ppermute | solution.py:15
  146.6 4.5 %collective-permute-start.15 = (f32[1,1,2,1,128]{4,2,3,1,0:T(2,128)S(1)}, f32[1,1,2,1,128]{4,2,3,1,0:T(2,128)S(1)}, u32[]{:S(2)}, u32[]{:S(2)}) collective-permute-start(f32[1,1,2,1,128]{4,2,3,1,0:T(2,128)S(1)} %multiply_bitcast_fusion.4), channel_id=1, source_target_pairs={{0,4},{1,5},{2,6},{3,7},{8,12},{9,13},{10,14},{11,15},{16,20},{17,... | collective-permute-start | bytes 3080 | tf_op jit(solution)/shard_map/ppermute | solution.py:15
  151.3 2.5 collective-permute-start.17
  154.4 0.3 fusion.33
  154.7 0.7 fusion.124
  155.4 42.2 %all-reduce.1 = (f32[32]{0:T(128)S(1)}, f32[]{:T(128)}, f32[]{:T(128)}) all-reduce(f32[32]{0:T(128)S(1)} %convolution_bitcast_fusion.2, f32[]{:T(128)} %get-tuple-element.6, f32[]{:T(128)} %get-tuple-element.5), channel_id=1, replica_groups=mesh['gx'=4,'gy'=2,'gz'=4] {'gx','gy','gz'}, use_global_device_ids=true, to_apply=%region_13.15 | all-reduce | flops 34 | bytes 272 | tf_op jit(solution)/shard_map/psum | solution.py:63
  197.7 0.7 fusion.139
  202.6 1.3 collective-permute-start.18
  203.9 1.3 collective-permute-start.20
  205.8 1.3 collective-permute-start.22
  207.2 4.5 %collective-permute-start.19 = (f32[1,1,2,1,128]{4,2,3,1,0:T(2,128)S(1)}, f32[1,1,2,1,128]{4,2,3,1,0:T(2,128)S(1)}, u32[]{:S(2)}, u32[]{:S(2)}) collective-permute-start(f32[1,1,2,1,128]{4,2,3,1,0:T(2,128)S(1)} %multiply_bitcast_fusion.2), channel_id=1, source_target_pairs={{0,8},{8,16},{16,24},{1,9},{9,17},{17,25},{2,10},{10,18},{18,26},{... | collective-permute-start | bytes 3080 | tf_op jit(solution)/shard_map/ppermute | solution.py:15
  211.8 4.5 %collective-permute-start.21 = (f32[1,1,2,1,128]{4,2,3,1,0:T(2,128)S(1)}, f32[1,1,2,1,128]{4,2,3,1,0:T(2,128)S(1)}, u32[]{:S(2)}, u32[]{:S(2)}) collective-permute-start(f32[1,1,2,1,128]{4,2,3,1,0:T(2,128)S(1)} %multiply_bitcast_fusion.1), channel_id=1, source_target_pairs={{0,4},{1,5},{2,6},{3,7},{8,12},{9,13},{10,14},{11,15},{16,20},{17,... | collective-permute-start | bytes 3080 | tf_op jit(solution)/shard_map/ppermute | solution.py:15
  216.4 2.5 collective-permute-start.23
  219.9 0.7 fusion.121
  220.6 41.0 %all-reduce = (f32[32]{0:T(128)S(1)}, f32[]{:T(128)}, f32[]{:T(128)}) all-reduce(f32[32]{0:T(128)S(1)} %convolution_bitcast_fusion.1, f32[]{:T(128)} %get-tuple-element.4, f32[]{:T(128)} %get-tuple-element.3), channel_id=1, replica_groups=mesh['gx'=4,'gy'=2,'gz'=4] {'gx','gy','gz'}, use_global_device_ids=true, to_apply=%region_18.20 | all-reduce | flops 34 | bytes 272 | tf_op jit(solution)/shard_map/psum | solution.py:63
  261.6 0.7 fusion.137
  265.9 0.6 bitcast_subtract_fusion
  (99 shorter events, 9.9 us)
Async XLA Ops:
  0.6 16.8 %copy-start = (f32[1,1,2,128,128]{4,3,2,1,0:T(8,128)S(1)}, f32[1,1,2,128,128]{4,3,2,1,0:T(8,128)}, u32[]{:S(2)}) copy-start(f32[1,1,2,128,128]{4,3,2,1,0:T(8,128)} %param.8) | copy-start | bytes 393220
  0.6 5.7 %copy-start.2 = (f32[1,1,2,32,128]{4,3,2,1,0:T(8,128)S(1)}, f32[1,1,2,32,128]{4,3,2,1,0:T(8,128)}, u32[]{:S(2)}) copy-start(f32[1,1,2,32,128]{4,3,2,1,0:T(8,128)} %param.11) | copy-start | bytes 98308
  0.7 16.6 %copy-start.1 = (f32[3,1,1,2,128,128]{5,4,3,2,1,0:T(8,128)S(1)}, f32[3,1,1,2,128,128]{5,4,3,2,1,0:T(8,128)}, u32[]{:S(2)}) copy-start(f32[3,1,1,2,128,128]{5,4,3,2,1,0:T(8,128)} %param.9) | copy-start | bytes 1179652
  0.7 22.8 %collective-permute-start.2 = (f32[1,1,2,32,128]{4,3,2,1,0:T(8,128)}, f32[1,1,2,32,128]{4,3,2,1,0:T(8,128)S(1)}, u32[]{:S(2)}, u32[]{:S(2)}) collective-permute-start(f32[1,1,2,32,128]{4,3,2,1,0:T(8,128)} %param.11), channel_id=1, source_target_pairs={{4,0},{5,1},{6,2},{7,3},{12,8},{13,9},{14,10},{15,11},{20,16},{21,... | collective-permute-start | bytes 98312 | tf_op jit(solution)/shard_map/ppermute | solution.py:15
  2.1 22.7 %collective-permute-start = (f32[1,1,2,32,128]{4,3,2,1,0:T(8,128)}, f32[1,1,2,32,128]{4,3,2,1,0:T(8,128)S(1)}, u32[]{:S(2)}, u32[]{:S(2)}) collective-permute-start(f32[1,1,2,32,128]{4,3,2,1,0:T(8,128)} %param.11), channel_id=1, source_target_pairs={{8,0},{16,8},{24,16},{9,1},{17,9},{25,17},{10,2},{18,10},{26,18},{... | collective-permute-start | bytes 98312 | tf_op jit(solution)/shard_map/ppermute | solution.py:15
  4.1 14.5 %collective-permute-start.4 = (f32[1,1,1,32,128]{4,3,2,1,0:T(8,128)S(1)}, f32[1,1,1,32,128]{4,3,2,1,0:T(8,128)S(1)}, u32[]{:S(2)}, u32[]{:S(2)}) collective-permute-start(f32[1,1,1,32,128]{4,3,2,1,0:T(8,128)S(1)} %get-tuple-element.31), channel_id=1, source_target_pairs={{1,0},{2,1},{3,2},{5,4},{6,5},{7,6},{9,8},{10,9},{11,10},{13,12},{... | collective-permute-start | bytes 49160 | tf_op jit(solution)/shard_map/ppermute | solution.py:15
  7.4 16.4 %collective-permute-start.5 = (f32[1,1,1,32,128]{4,3,2,1,0:T(8,128)S(1)}, f32[1,1,1,32,128]{4,3,2,1,0:T(8,128)S(1)}, u32[]{:S(2)}, u32[]{:S(2)}) collective-permute-start(f32[1,1,1,32,128]{4,3,2,1,0:T(8,128)S(1)} %get-tuple-element.28), channel_id=1, source_target_pairs={{0,1},{1,2},{2,3},{4,5},{5,6},{6,7},{8,9},{9,10},{10,11},{12,13},{... | collective-permute-start | bytes 49160 | tf_op jit(solution)/shard_map/ppermute | solution.py:15
  11.6 12.2 %collective-permute-start.1 = (f32[1,1,2,32,128]{4,3,2,1,0:T(8,128)S(1)}, f32[1,1,2,32,128]{4,3,2,1,0:T(8,128)S(1)}, u32[]{:S(2)}, u32[]{:S(2)}) collective-permute-start(f32[1,1,2,32,128]{4,3,2,1,0:T(8,128)S(1)} %fusion.4), channel_id=1, source_target_pairs={{0,8},{8,16},{16,24},{1,9},{9,17},{17,25},{2,10},{10,18},{18,26},{... | collective-permute-start | bytes 98312 | tf_op jit(solution)/shard_map/ppermute | solution.py:15
  17.8 0.7 copy-start.3
  18.6 6.1 %collective-permute-start.3 = (f32[1,1,2,32,128]{4,3,2,1,0:T(8,128)S(1)}, f32[1,1,2,32,128]{4,3,2,1,0:T(8,128)S(1)}, u32[]{:S(2)}, u32[]{:S(2)}) collective-permute-start(f32[1,1,2,32,128]{4,3,2,1,0:T(8,128)S(1)} %fusion.2), channel_id=1, source_target_pairs={{0,4},{1,5},{2,6},{3,7},{8,12},{9,13},{10,14},{11,15},{16,20},{17,... | collective-permute-start | bytes 98312 | tf_op jit(solution)/shard_map/ppermute | solution.py:15
  75.3 16.4 %collective-permute-start.6 = (f32[1,1,2,1,128]{4,2,3,1,0:T(2,128)S(1)}, f32[1,1,2,1,128]{4,2,3,1,0:T(2,128)S(1)}, u32[]{:S(2)}, u32[]{:S(2)}) collective-permute-start(f32[1,1,2,1,128]{4,2,3,1,0:T(2,128)S(1)} %bitcast.524), channel_id=1, source_target_pairs={{8,0},{16,8},{24,16},{9,1},{17,9},{25,17},{10,2},{18,10},{26,18},{... | collective-permute-start | bytes 3080 | tf_op jit(solution)/shard_map/ppermute | solution.py:15
  76.6 15.5 %collective-permute-start.8 = (f32[1,1,2,1,128]{4,2,3,1,0:T(2,128)S(1)}, f32[1,1,2,1,128]{4,2,3,1,0:T(2,128)S(1)}, u32[]{:S(2)}, u32[]{:S(2)}) collective-permute-start(f32[1,1,2,1,128]{4,2,3,1,0:T(2,128)S(1)} %bitcast.525), channel_id=1, source_target_pairs={{4,0},{5,1},{6,2},{7,3},{12,8},{13,9},{14,10},{15,11},{20,16},{21,... | collective-permute-start | bytes 3080 | tf_op jit(solution)/shard_map/ppermute | solution.py:15
  78.3 10.6 %collective-permute-start.10 = (f32[1,1,1,1,128]{4,2,3,1,0:T(1,128)S(1)}, f32[1,1,1,1,128]{4,2,3,1,0:T(1,128)S(1)}, u32[]{:S(2)}, u32[]{:S(2)}) collective-permute-start(f32[1,1,1,1,128]{4,2,3,1,0:T(1,128)S(1)} %get-tuple-element.43), channel_id=1, source_target_pairs={{1,0},{2,1},{3,2},{5,4},{6,5},{7,6},{9,8},{10,9},{11,10},{13,12},{... | collective-permute-start | bytes 1544 | tf_op jit(solution)/shard_map/ppermute | solution.py:15
  79.7 12.7 %collective-permute-start.7 = (f32[1,1,2,1,128]{4,2,3,1,0:T(2,128)S(1)}, f32[1,1,2,1,128]{4,2,3,1,0:T(2,128)S(1)}, u32[]{:S(2)}, u32[]{:S(2)}) collective-permute-start(f32[1,1,2,1,128]{4,2,3,1,0:T(2,128)S(1)} %multiply_bitcast_fusion.8), channel_id=1, source_target_pairs={{0,8},{8,16},{16,24},{1,9},{9,17},{17,25},{2,10},{10,18},{18,26},{... | collective-permute-start | bytes 3080 | tf_op jit(solution)/shard_map/ppermute | solution.py:15
  84.3 8.1 %collective-permute-start.9 = (f32[1,1,2,1,128]{4,2,3,1,0:T(2,128)S(1)}, f32[1,1,2,1,128]{4,2,3,1,0:T(2,128)S(1)}, u32[]{:S(2)}, u32[]{:S(2)}) collective-permute-start(f32[1,1,2,1,128]{4,2,3,1,0:T(2,128)S(1)} %multiply_bitcast_fusion.7), channel_id=1, source_target_pairs={{0,4},{1,5},{2,6},{3,7},{8,12},{9,13},{10,14},{11,15},{16,20},{17,... | collective-permute-start | bytes 3080 | tf_op jit(solution)/shard_map/ppermute | solution.py:15
  88.9 3.4 %collective-permute-start.11 = (f32[1,1,1,1,128]{4,2,3,1,0:T(1,128)S(1)}, f32[1,1,1,1,128]{4,2,3,1,0:T(1,128)S(1)}, u32[]{:S(2)}, u32[]{:S(2)}) collective-permute-start(f32[1,1,1,1,128]{4,2,3,1,0:T(1,128)S(1)} %get-tuple-element.44), channel_id=1, source_target_pairs={{0,1},{1,2},{2,3},{4,5},{5,6},{6,7},{8,9},{9,10},{10,11},{12,13},{... | collective-permute-start | bytes 1544 | tf_op jit(solution)/shard_map/ppermute | solution.py:15
  137.5 16.6 %collective-permute-start.12 = (f32[1,1,2,1,128]{4,2,3,1,0:T(2,128)S(1)}, f32[1,1,2,1,128]{4,2,3,1,0:T(2,128)S(1)}, u32[]{:S(2)}, u32[]{:S(2)}) collective-permute-start(f32[1,1,2,1,128]{4,2,3,1,0:T(2,128)S(1)} %bitcast.531), channel_id=1, source_target_pairs={{8,0},{16,8},{24,16},{9,1},{17,9},{25,17},{10,2},{18,10},{26,18},{... | collective-permute-start | bytes 3080 | tf_op jit(solution)/shard_map/ppermute | solution.py:15
  138.8 15.6 %collective-permute-start.14 = (f32[1,1,2,1,128]{4,2,3,1,0:T(2,128)S(1)}, f32[1,1,2,1,128]{4,2,3,1,0:T(2,128)S(1)}, u32[]{:S(2)}, u32[]{:S(2)}) collective-permute-start(f32[1,1,2,1,128]{4,2,3,1,0:T(2,128)S(1)} %bitcast.532), channel_id=1, source_target_pairs={{4,0},{5,1},{6,2},{7,3},{12,8},{13,9},{14,10},{15,11},{20,16},{21,... | collective-permute-start | bytes 3080 | tf_op jit(solution)/shard_map/ppermute | solution.py:15
  140.6 10.6 %collective-permute-start.16 = (f32[1,1,1,1,128]{4,2,3,1,0:T(1,128)S(1)}, f32[1,1,1,1,128]{4,2,3,1,0:T(1,128)S(1)}, u32[]{:S(2)}, u32[]{:S(2)}) collective-permute-start(f32[1,1,1,1,128]{4,2,3,1,0:T(1,128)S(1)} %get-tuple-element.39), channel_id=1, source_target_pairs={{1,0},{2,1},{3,2},{5,4},{6,5},{7,6},{9,8},{10,9},{11,10},{13,12},{... | collective-permute-start | bytes 1544 | tf_op jit(solution)/shard_map/ppermute | solution.py:15
  142.0 12.7 %collective-permute-start.13 = (f32[1,1,2,1,128]{4,2,3,1,0:T(2,128)S(1)}, f32[1,1,2,1,128]{4,2,3,1,0:T(2,128)S(1)}, u32[]{:S(2)}, u32[]{:S(2)}) collective-permute-start(f32[1,1,2,1,128]{4,2,3,1,0:T(2,128)S(1)} %multiply_bitcast_fusion.5), channel_id=1, source_target_pairs={{0,8},{8,16},{16,24},{1,9},{9,17},{17,25},{2,10},{10,18},{18,26},{... | collective-permute-start | bytes 3080 | tf_op jit(solution)/shard_map/ppermute | solution.py:15
  146.6 8.1 %collective-permute-start.15 = (f32[1,1,2,1,128]{4,2,3,1,0:T(2,128)S(1)}, f32[1,1,2,1,128]{4,2,3,1,0:T(2,128)S(1)}, u32[]{:S(2)}, u32[]{:S(2)}) collective-permute-start(f32[1,1,2,1,128]{4,2,3,1,0:T(2,128)S(1)} %multiply_bitcast_fusion.4), channel_id=1, source_target_pairs={{0,4},{1,5},{2,6},{3,7},{8,12},{9,13},{10,14},{11,15},{16,20},{17,... | collective-permute-start | bytes 3080 | tf_op jit(solution)/shard_map/ppermute | solution.py:15
  151.3 3.4 %collective-permute-start.17 = (f32[1,1,1,1,128]{4,2,3,1,0:T(1,128)S(1)}, f32[1,1,1,1,128]{4,2,3,1,0:T(1,128)S(1)}, u32[]{:S(2)}, u32[]{:S(2)}) collective-permute-start(f32[1,1,1,1,128]{4,2,3,1,0:T(1,128)S(1)} %get-tuple-element.40), channel_id=1, source_target_pairs={{0,1},{1,2},{2,3},{4,5},{5,6},{6,7},{8,9},{9,10},{10,11},{12,13},{... | collective-permute-start | bytes 1544 | tf_op jit(solution)/shard_map/ppermute | solution.py:15
  202.6 16.6 %collective-permute-start.18 = (f32[1,1,2,1,128]{4,2,3,1,0:T(2,128)S(1)}, f32[1,1,2,1,128]{4,2,3,1,0:T(2,128)S(1)}, u32[]{:S(2)}, u32[]{:S(2)}) collective-permute-start(f32[1,1,2,1,128]{4,2,3,1,0:T(2,128)S(1)} %bitcast.539), channel_id=1, source_target_pairs={{8,0},{16,8},{24,16},{9,1},{17,9},{25,17},{10,2},{18,10},{26,18},{... | collective-permute-start | bytes 3080 | tf_op jit(solution)/shard_map/ppermute | solution.py:15
  203.9 15.6 %collective-permute-start.20 = (f32[1,1,2,1,128]{4,2,3,1,0:T(2,128)S(1)}, f32[1,1,2,1,128]{4,2,3,1,0:T(2,128)S(1)}, u32[]{:S(2)}, u32[]{:S(2)}) collective-permute-start(f32[1,1,2,1,128]{4,2,3,1,0:T(2,128)S(1)} %bitcast.540), channel_id=1, source_target_pairs={{4,0},{5,1},{6,2},{7,3},{12,8},{13,9},{14,10},{15,11},{20,16},{21,... | collective-permute-start | bytes 3080 | tf_op jit(solution)/shard_map/ppermute | solution.py:15
  205.8 10.6 %collective-permute-start.22 = (f32[1,1,1,1,128]{4,2,3,1,0:T(1,128)S(1)}, f32[1,1,1,1,128]{4,2,3,1,0:T(1,128)S(1)}, u32[]{:S(2)}, u32[]{:S(2)}) collective-permute-start(f32[1,1,1,1,128]{4,2,3,1,0:T(1,128)S(1)} %get-tuple-element.35), channel_id=1, source_target_pairs={{1,0},{2,1},{3,2},{5,4},{6,5},{7,6},{9,8},{10,9},{11,10},{13,12},{... | collective-permute-start | bytes 1544 | tf_op jit(solution)/shard_map/ppermute | solution.py:15
  207.2 12.7 %collective-permute-start.19 = (f32[1,1,2,1,128]{4,2,3,1,0:T(2,128)S(1)}, f32[1,1,2,1,128]{4,2,3,1,0:T(2,128)S(1)}, u32[]{:S(2)}, u32[]{:S(2)}) collective-permute-start(f32[1,1,2,1,128]{4,2,3,1,0:T(2,128)S(1)} %multiply_bitcast_fusion.2), channel_id=1, source_target_pairs={{0,8},{8,16},{16,24},{1,9},{9,17},{17,25},{2,10},{10,18},{18,26},{... | collective-permute-start | bytes 3080 | tf_op jit(solution)/shard_map/ppermute | solution.py:15
  211.8 8.1 %collective-permute-start.21 = (f32[1,1,2,1,128]{4,2,3,1,0:T(2,128)S(1)}, f32[1,1,2,1,128]{4,2,3,1,0:T(2,128)S(1)}, u32[]{:S(2)}, u32[]{:S(2)}) collective-permute-start(f32[1,1,2,1,128]{4,2,3,1,0:T(2,128)S(1)} %multiply_bitcast_fusion.1), channel_id=1, source_target_pairs={{0,4},{1,5},{2,6},{3,7},{8,12},{9,13},{10,14},{11,15},{16,20},{17,... | collective-permute-start | bytes 3080 | tf_op jit(solution)/shard_map/ppermute | solution.py:15
  216.4 3.4 %collective-permute-start.23 = (f32[1,1,1,1,128]{4,2,3,1,0:T(1,128)S(1)}, f32[1,1,1,1,128]{4,2,3,1,0:T(1,128)S(1)}, u32[]{:S(2)}, u32[]{:S(2)}) collective-permute-start(f32[1,1,1,1,128]{4,2,3,1,0:T(1,128)S(1)} %get-tuple-element.36), channel_id=1, source_target_pairs={{0,1},{1,2},{2,3},{4,5},{5,6},{6,7},{8,9},{9,10},{10,11},{12,13},{... | collective-permute-start | bytes 1544 | tf_op jit(solution)/shard_map/ppermute | solution.py:15
where the time goes:
time: 268 us; the launch traced here: 266 us
  blocking collectives  166 us (62%)
  starting transfers between devices  63.4 us (24%)
  matrix products  14.2 us (5%)
  other arithmetic  10.7 us (4%)
  between operations  9.62 us (4%)
    psum x3, blocking collectives, joint_of(): return lax.psum((local_sq, local_cross, local_proj), ('gx', 'gy', 'gz'))  124 us
    ppermute x24, starting transfers between devices, shifted(): return lax.ppermute(block, axis, route)  63.4 us
    psum x1, blocking collectives, per_device(): lax.psum((local_coarse, local_right), ('gx', 'gy', 'gz'))  41.9 us
  transfers between devices with their start and end apart: 24, of which 1 were waited for; matrix products, arithmetic and copies ran while one was open for 4% of the time, Pallas kernels for 0%

commit v1 on v0

v1 whole, which is shorter than its diff:
```python
import functools
import math

import jax
import jax.numpy as jnp
from jax import lax
from jax.experimental import pallas as pl
from jax.experimental.pallas import tpu as pltpu
from jax.sharding import PartitionSpec as P

ITERS = 3
AXES = ("gx", "gy", "gz")
COARSE_GROUPS = (("gy", "gz"), ("gx",))
DOT_GROUPS = (("gx", "gy", "gz"),)
MESH = pl.DeviceIdType.MESH
F32 = jnp.float32
BF16 = jnp.bfloat16


def place(index, group, sizes):
    coords = {}
    for axis in reversed(group):
        coords[axis] = lax.rem(index, sizes[axis])
        index = lax.div(index, sizes[axis])
    return coords


def position(group, sizes):
    index = 0
    for axis in group:
        index = index * sizes[axis] + lax.axis_index(axis)
    return index


def extent(group, sizes):
    return math.prod(sizes[axis] for axis in group)


def for_peers(group, sizes, action):
    count = extent(group, sizes)
    me = position(group, sizes)

    def body(k, carry):
        action(place(lax.rem(me + k, count), group, sizes))
        return carry

    lax.fori_loop(1, count, body, 0)


def split_rows(v):
    high = v.astype(BF16).astype(F32)
    rest = v - high
    middle = rest.astype(BF16).astype(F32)
    low = rest - middle
    if v.shape[0] == 1:
        row = lax.broadcasted_iota(jnp.int32, (8, v.shape[1]), 0)
        parts = jnp.where(row == 0, high, jnp.where(row == 1, middle, jnp.where(row == 2, low, 0.0)))
    else:
        parts = jnp.concatenate([high, middle, low], axis=0)
    return parts.astype(BF16)


def join_rows(out, rows):
    return out[:rows] + (out[rows : 2 * rows] + out[2 * rows : 3 * rows])


def split_pair(m):
    high = m.astype(BF16)
    return high, (m - high.astype(F32)).astype(BF16)


def times(v, high, low):
    parts = split_rows(v)
    out = jnp.dot(parts, high, preferred_element_type=F32)
    out = out + jnp.dot(parts, low, preferred_element_type=F32)
    return join_rows(out, v.shape[0])


def times_t(v, high, low):
    parts = split_rows(v)
    dims = (((1,), (1,)), ((), ()))
    out = lax.dot_general(parts, high, dims, preferred_element_type=F32)
    out = out + lax.dot_general(parts, low, dims, preferred_element_type=F32)
    return join_rows(out, v.shape[0])


def kernel(sizes, lz, block, defl, *refs):
    (right_ref, diag_ref, coup_ref, pat_ref, defl_ref, sol_ref, res_ref) = refs[:7]
    (loc_h, loc_l, out_h, out_l, in_h, in_l, zo_h, zo_l, zi_h, zi_l, proj_h, proj_l) = refs[7:19]
    n_ops = 1 + ITERS
    at = 19
    ops = []
    for _ in range(n_ops):
        ops.append(refs[at : at + 9])
        at += 9
    coarse_bufs = refs[at : at + len(COARSE_GROUPS)]
    at += len(COARSE_GROUPS)
    dot_bufs = [refs[at + k * len(DOT_GROUPS) : at + (k + 1) * len(DOT_GROUPS)] for k in range(ITERS)]
    at += ITERS * len(DOT_GROUPS)
    halo_send, halo_recv, red_send, red_recv = refs[at : at + 4]

    idx = {axis: lax.axis_index(axis) for axis in AXES}
    lower = {axis: idx[axis] > 0 for axis in AXES}
    upper = {axis: idx[axis] < sizes[axis] - 1 for axis in AXES}
    barrier = pltpu.get_barrier_semaphore()

    for op in ops:
        for ref in op[4:9]:
            ref[...] = jnp.zeros_like(ref)
        op[3][...] = jnp.zeros_like(op[3])

    def greet(peer):
        pl.semaphore_signal(barrier, inc=1, device_id=peer, device_id_type=MESH)

    for_peers(AXES, sizes, greet)

    def gate(d, c):
        return pat_ref[d, 0, 0, c].astype(F32)

    def put(ref_h, ref_l, rows, cols, value):
        high, low = split_pair(value)
        ref_h[rows, cols] = high
        ref_l[rows, cols] = low

    def span(c):
        return slice(c * block, (c + 1) * block)

    if lz > 2:
        loc_h[...] = jnp.zeros_like(loc_h)
        loc_l[...] = jnp.zeros_like(loc_l)
    for c in range(lz):
        put(loc_h, loc_l, span(c), span(c), diag_ref[0, 0, c])
        cx = gate(0, c) * coup_ref[0, 0, 0, c]
        cy = gate(1, c) * coup_ref[1, 0, 0, c]
        cz = gate(2, c) * coup_ref[2, 0, 0, c]
        put(out_h.at[c], out_l.at[c], slice(None), span(0), cx)
        put(out_h.at[c], out_l.at[c], slice(None), span(1), cy)
        put(in_h.at[c], in_l.at[c], span(0), slice(None), cx.T)
        put(in_h.at[c], in_l.at[c], span(1), slice(None), cy.T)
        if c + 1 < lz:
            put(loc_h, loc_l, span(c), span(c + 1), cz)
            put(loc_h, loc_l, span(c + 1), span(c), cz.T)
        else:
            put(zo_h, zo_l, slice(None), slice(None), cz)
            put(zi_h, zi_l, slice(None), slice(None), cz.T)

    right = jnp.concatenate([right_ref[0, 0, c : c + 1, :] for c in range(lz)], axis=1)
    basis = jnp.concatenate([defl_ref[0, 0, c] for c in range(lz)], axis=1)

    def halo_copies(k):
        field, car_x, car_y, car_z, bey_x, bey_y, bey_z, arr_xy, arr_z = ops[k]
        routes = (
            ("gx", -1, field, bey_x),
            ("gy", -1, field, bey_y),
            ("gz", -1, field.at[0], bey_z),
            ("gx", 1, car_x, arr_xy.at[0]),
            ("gy", 1, car_y, arr_xy.at[1]),
            ("gz", 1, car_z, arr_z),
        )
        copies = []
        for j, (axis, way, src, dst) in enumerate(routes):
            copies.append(
                (
                    lower[axis] if way < 0 else upper[axis],
                    upper[axis] if way < 0 else lower[axis],
                    pltpu.make_async_remote_copy(
                        src_ref=src,
                        dst_ref=dst,
                        send_sem=halo_send.at[k, j],
                        recv_sem=halo_recv.at[k, j],
                        device_id={axis: jnp.clip(idx[axis] + way, 0, sizes[axis] - 1)},
                        device_id_type=MESH,
                    ),
                )
            )
        return copies

    def start(copies):
        for sends, _, copy in copies:
            pl.when(sends)(copy.start)

    def open_product(k, v):
        field, car_x, car_y, car_z = ops[k][:4]
        copies = halo_copies(k)
        for c in range(lz):
            field[c] = v[:, span(c)]
        start(copies[:3])
        for c in range(lz):
            carried = times(v[:, span(c)], out_h[c], out_l[c])
            car_x[c] = carried[:, span(0)]
            car_y[c] = carried[:, span(1)]
        car_z[...] = times(v[:, span(lz - 1)], zo_h[...], zo_l[...])
        start(copies[3:])
        return times(v, loc_h[...], loc_l[...])

    def close_product(k, own):
        _, _, _, _, bey_x, bey_y, bey_z, arr_xy, arr_z = ops[k]
        for _, comes, copy in halo_copies(k):
            pl.when(comes)(copy.wait_recv)
        parts = []
        for c in range(lz):
            beyond = jnp.concatenate([bey_x[c], bey_y[c]], axis=1)
            part = times(beyond, in_h[c], in_l[c])
            part = part + arr_xy[0, c] + arr_xy[1, c]
            if c == 0:
                part = part + arr_z[...]
            if c == lz - 1:
                part = part + times(bey_z[...], zi_h[...], zi_l[...])
            parts.append(part)
        return own + jnp.concatenate(parts, axis=1)

    def gathered(buf, sem):
        rest = buf.at[pl.ds(0, buf.shape[0] - 1)]
        return pltpu.make_async_copy(rest, rest, sem)

    def reduce_start(buf, group, sem, value):
        me = position(group, sizes)
        buf[me] = value
        own = buf.at[me]

        def send(peer):
            pltpu.make_async_remote_copy(
                src_ref=own,
                dst_ref=own,
                send_sem=red_send.at[sem],
                recv_sem=red_recv.at[sem],
                device_id=peer,
                device_id_type=MESH,
            ).start()

        for_peers(group, sizes, send)

    def reduce_done(buf, sem):
        gathered(buf, red_recv.at[sem]).wait()
        return jnp.sum(buf[...], axis=0)

    def spread(coef, fields):
        return jnp.sum(coef * fields, axis=0, keepdims=True)

    rows_first = ops[0][0].shape[1]
    first = jnp.concatenate([basis, right, jnp.zeros((rows_first - defl - 1, lz * block), F32)], axis=0)
    pl.semaphore_wait(barrier, extent(AXES, sizes) - 1)
    own = open_product(0, first)
    proj_h[...] = jnp.zeros_like(proj_h)
    proj_l[...] = jnp.zeros_like(proj_l)
    everything = slice(None)
    put(proj_h, proj_l, slice(0, defl), everything, basis)
    right_local = times_t(right, proj_h[...], proj_l[...])
    both = close_product(0, own)
    applied = both[:defl]
    image = both[defl : defl + 1]

    reps = block // defl
    apart = defl // reps
    for g in range(reps):
        put(proj_h, proj_l, slice(g * defl, (g + 1) * defl), everything, applied)
    coarse_local = times_t(basis, proj_h[...], proj_l[...])
    lane = lax.broadcasted_iota(jnp.int32, (apart, block), 1)
    packed = jnp.zeros((apart, block), F32)
    for g in range(reps):
        inside = (lane >= g * defl) & (lane < (g + 1) * defl)
        packed = packed + jnp.where(inside, coarse_local[g * apart : (g + 1) * apart], 0.0)
    sem = 0
    value = jnp.concatenate([packed, jnp.broadcast_to(right_local, (8, block))], axis=0)
    reduce_start(coarse_bufs[0], COARSE_GROUPS[0], sem, value)
    own = open_product(1, applied)
    put(proj_h, proj_l, slice(defl, block), everything, jnp.zeros((block - defl, lz * block), F32))
    for k in range(1, len(COARSE_GROUPS)):
        value = reduce_done(coarse_bufs[k - 1], sem)
        sem += 1
        reduce_start(coarse_bufs[k], COARSE_GROUPS[k], sem, value)
    value = reduce_done(coarse_bufs[-1], sem)
    sem += 1
    coarse = jnp.concatenate(
        [value[:apart]] + [pltpu.roll(value[:apart], block - g * defl, 1) for g in range(1, reps)], axis=0
    )
    col = lax.broadcasted_iota(jnp.int32, (defl, block), 1)
    row = lax.broadcasted_iota(jnp.int32, (defl, block), 0)
    coarse = jnp.where(col < defl, coarse, 0.0)
    square = jnp.concatenate([coarse, jnp.zeros((block - defl, block), F32)], axis=0)
    inv = 0.5 * (coarse + square.T[:defl])
    for k in range(defl):
        pivot = 1.0 / inv[k : k + 1, k : k + 1]
        line = jnp.where(col[:1] == k, pivot, inv[k : k + 1] * pivot)
        inv = jnp.where(row == k, line, jnp.where(col == k, 0.0, inv) - inv[:, k : k + 1] * line)
    eye = jnp.where(row == col, 1.0, 0.0)

    def coarse_solve(projected):
        return jnp.sum(inv * projected, axis=1, keepdims=True)

    twice = close_product(1, own)
    coef = coarse_solve(value[apart : apart + 1])
    x = spread(coef, basis)
    r = right - spread(coef, applied)
    w = image - spread(coef, twice)
    d = s = z = curv = norm = None
    lane_row = lax.broadcasted_iota(jnp.int32, (1, block), 1)
    for it in range(ITERS):
        last = it + 1 == ITERS
        local = times_t(r, proj_h[...], proj_l[...])
        sq = jnp.sum(r * r, axis=1, keepdims=True)
        cross = jnp.sum(r * w, axis=1, keepdims=True)
        local = jnp.where(lane_row == defl, sq, jnp.where(lane_row == defl + 1, cross, local))
        bufs = dot_bufs[it]
        reduce_start(bufs[0], DOT_GROUPS[0], sem, local)
        if not last:
            own = open_product(2 + it, w)
        for k in range(1, len(DOT_GROUPS)):
            local = reduce_done(bufs[k - 1], sem)
            sem += 1
            reduce_start(bufs[k], DOT_GROUPS[k], sem, local)
        if not last:
            q = close_product(2 + it, own)
        total = reduce_done(bufs[-1], sem)
        sem += 1
        coef = coarse_solve(total)
        mine = jnp.sum(eye * total, axis=1, keepdims=True)
        energy = jnp.sum(mine * coef, axis=0, keepdims=True)
        norm_new = total[:, defl : defl + 1]
        cross = total[:, defl + 1 : defl + 2]
        if it == 0:
            d = r - spread(coef, basis)
            s = w - spread(coef, applied)
            z = q - spread(coef, twice)
            curv = cross - energy
        else:
            growth = norm_new / norm
            d = r + growth * d - spread(coef, basis)
            s = w + growth * s - spread(coef, applied)
            if not last:
                z = q + growth * z - spread(coef, twice)
            curv = cross - growth * growth * curv - energy
        norm = norm_new
        step = norm / curv
        x = x + step * d
        r = r - step * s
        if not last:
            w = w - step * z
    for c in range(lz):
        sol_ref[0, 0, c : c + 1, :] = x[:, span(c)]
        res_ref[0, 0, c : c + 1, :] = r[:, span(c)]

    for k in range(n_ops):
        for sends, _, copy in halo_copies(k):
            pl.when(sends)(copy.wait_send)
    every = list(coarse_bufs) + [buf for bufs in dot_bufs for buf in bufs]
    for k, buf in enumerate(every):
        gathered(buf, red_send.at[k]).wait()


def solution(mesh):
    sizes = dict(mesh.shape)
    in_specs = (
        P("gx", "gy", "gz", None),
        P("gx", "gy", "gz", None, None),
        P(None, "gx", "gy", "gz", None, None),
        P(None, "gx", "gy", "gz"),
        P("gx", "gy", "gz", None, None),
    )
    out_specs = (P("gx", "gy", "gz", None), P("gx", "gy", "gz", None))

    def per_device(right_side, diag_blocks, couplings, pattern, deflation):
        lx, ly, lz, block = right_side.shape
        assert lx == 1 and ly == 1
        defl = deflation.shape[3]
        rows_first = (defl + 1 + 7) // 8 * 8
        wide = lz * block
        scratch = []
        for shape in (
            (wide, wide),
            (lz, block, 2 * block),
            (lz, 2 * block, block),
            (block, block),
            (block, block),
            (block, wide),
        ):
            scratch += [pltpu.VMEM(shape, BF16)] * 2
        for rows in (rows_first, defl) + (1,) * (ITERS - 1):
            layer, face = (lz, rows, block), (rows, block)
            scratch += [pltpu.VMEM(layer, F32)] * 3 + [pltpu.VMEM(face, F32)]
            scratch += [pltpu.VMEM(layer, F32)] * 2 + [pltpu.VMEM(face, F32)]
            scratch += [pltpu.VMEM((2,) + layer, F32), pltpu.VMEM(face, F32)]
        for group in COARSE_GROUPS:
            scratch.append(pltpu.VMEM((extent(group, sizes), defl * defl // block + 8, block), F32))
        for _ in range(ITERS):
            for group in DOT_GROUPS:
                scratch.append(pltpu.VMEM((extent(group, sizes), 1, block), F32))
        reductions = len(COARSE_GROUPS) + ITERS * len(DOT_GROUPS)
        scratch += [pltpu.SemaphoreType.DMA((1 + ITERS, 6))] * 2
        scratch += [pltpu.SemaphoreType.DMA((reductions,))] * 2
        vmem = pl.BlockSpec(memory_space=pltpu.VMEM)
        smem = pl.BlockSpec(memory_space=pltpu.SMEM)
        out = jax.ShapeDtypeStruct(right_side.shape, F32)
        return pl.pallas_call(
            functools.partial(kernel, sizes, lz, block, defl),
            out_shape=(out, out),
            in_specs=[vmem, vmem, vmem, smem, vmem],
            out_specs=(vmem, vmem),
            scratch_shapes=scratch,
            compiler_params=pltpu.CompilerParams(
                collective_id=0, has_side_effects=True, vmem_limit_bytes=48 * 1024 * 1024
            ),
        )(right_side, diag_blocks, couplings, pattern, deflation)

    return jax.shard_map(
        per_device, mesh=mesh, in_specs=in_specs, out_specs=out_specs, check_vma=False
    )
```

time: 268 us -> 41.9 us (0.16)
  blocking collectives: 166 us -> 0 us
  starting transfers between devices: 63.4 us -> 0 us
  Pallas kernels: 0 us -> 36.4 us
  matrix products: 14.2 us -> 0 us
  other arithmetic: 10.7 us -> 0 us
  between operations: 9.62 us -> 0.65 us
  local copies, waits for them, and re-layouts: 1.82 us -> 4.56 us
    psum x4 -> x0, blocking collectives: 166 us -> none  [the longest x3 124 us: joint_of(): return lax.psum((local_sq, local_cross, local_proj), ('gx', 'gy', 'gz'))]
    ppermute x24 -> x0, starting transfers between devices: 63.4 us -> none  [shifted(): return lax.ppermute(block, axis, route)]
    pallas_call x0 -> x1, Pallas kernels: none -> 36.4 us  [per_device(): pl.pallas_call(functools.partial(kernel, sizes, lz, block, defl), out_sha...]
    dot_general x41 -> x0, matrix products: 11.2 us -> none  [the longest x16 4.98 us: rows_times(): return jnp.einsum('xyzrk,xyzck->xyzcr', blocks, vectors, precision=HIGHEST)]
    another operation x5 -> x0, other arithmetic: 6.69 us -> none  [the longest x3 3.6 us: per_device(): factor = jnp.linalg.cholesky(coarse_mat)]
    unnamed x8 -> x11, local copies, waits for them, and re-layouts: 0.72 us -> 4.56 us
    another operation x8 -> x0, matrix products: 3.02 us -> none  [per_device(): coarse_coef = jax.scipy.linalg.cho_solve((factor, True), projected)]
  transfers between devices with their start and end apart: 24 -> 0, of which waited for: 1 -> 0; matrix products, arithmetic and copies ran while one was open for 4% -> 0% of each run, Pallas kernels for 0% -> 0%
where the time goes in v1:
time: 41.9 us; the launch traced here: 41.6 us
  Pallas kernels  36.4 us (87%)
  local copies, waits for them, and re-layouts  4.56 us (11%)
  between operations  0.65 us (2%)
    pallas_call x1, Pallas kernels, per_device(): pl.pallas_call(functools.partial(kernel, sizes, lz, block, defl), out_sha...  36.4 us
    unnamed x11, local copies, waits for them, and re-layouts  4.56 us

profile of v1, /device:TPU:0, one launch (start us, length us, event | category | flops | bytes accessed | tf_op | source)
XLA Modules:
  0.0 41.6 jit_solution(6164912400993362883)
XLA Ops:
  0.6 0.0 copy-start.3
  0.6 0.8 %copy.7.refs_3_ = s32[3,1,1,2]{3,2,1,0:T(1,128)S(1)} copy(s32[3,1,1,2]{0,3,2,1:T(2,128)} %param.8) | data formatting | bytes 48 | tf_op args[3]
  1.4 0.0 copy-done.3
  1.4 0.0 copy-start
  1.4 1.0 %copy-done = f32[3,1,1,2,128,128]{5,4,3,2,1,0:T(8,128)S(1)} copy-done((f32[3,1,1,2,128,128]{5,4,3,2,1,0:T(8,128)S(1)}, f32[3,1,1,2,128,128]{5,4,3,2,1,0:T(8,128)}, u32[]{:S(2)}) %copy-start) | copy-done | bytes 393240
  2.4 0.0 copy-start.1
  2.4 0.9 %copy-done.1 = f32[1,1,2,128,128]{4,3,2,1,0:T(8,128)S(1)} copy-done((f32[1,1,2,128,128]{4,3,2,1,0:T(8,128)S(1)}, f32[1,1,2,128,128]{4,3,2,1,0:T(8,128)}, u32[]{:S(2)}) %copy-start.1) | copy-done | bytes 131096
  3.3 0.0 copy-start.2
  3.3 0.8 %copy-done.2 = f32[1,1,2,32,128]{4,3,2,1,0:T(8,128)S(1)} copy-done((f32[1,1,2,32,128]{4,3,2,1,0:T(8,128)S(1)}, f32[1,1,2,32,128]{4,3,2,1,0:T(8,128)}, u32[]{:S(2)}) %copy-start.2) | copy-done | bytes 32792
  4.1 36.4 %shard_map.68 = (f32[1,1,2,128]{3,2,1,0:T(2,128)S(1)}, f32[1,1,2,128]{3,2,1,0:T(2,128)S(1)}) custom-call(f32[1,1,2,128]{3,2,1,0:T(2,128)S(1)} %copy-done.3, f32[1,1,2,128,128]{4,3,2,1,0:T(8,128)S(1)} %copy-done.1, f32[3,1,1,2,128,128]{5,4,3,2,1,0:T(8,128)S(1)} %copy-done, s32[3,1,1,2]{3,2,1,0:T(1,128)S(1)} %copy.7.refs_3_, f32[1,1,2,32,128]{4,3,2,1,0:T(8,128)S(1)} %copy-done.2), custom_call_target="tpu_custom_call" | custom-call | tf_op jit(solution)/shard_map/pallas_call | solution.py:394
  40.5 0.6 %copy.10 = f32[1,1,2,128]{3,2,1,0:T(2,128)} copy(f32[1,1,2,128]{3,2,1,0:T(2,128)S(1)} %get-tuple-element.4) | data formatting | bytes 2048
  41.1 0.6 %copy.11 = f32[1,1,2,128]{3,2,1,0:T(2,128)} copy(f32[1,1,2,128]{3,2,1,0:T(2,128)S(1)} %get-tuple-element.5) | data formatting | bytes 2048
Async XLA Ops:
  0.6 0.8 %copy-start.3 = (f32[1,1,2,128]{3,2,1,0:T(2,128)S(1)}, f32[1,1,2,128]{3,2,1,0:T(2,128)}, u32[]{:S(2)}) copy-start(f32[1,1,2,128]{3,2,1,0:T(2,128)} %refs_0_.1) | copy-start | bytes 3076
  1.4 1.0 %copy-start = (f32[3,1,1,2,128,128]{5,4,3,2,1,0:T(8,128)S(1)}, f32[3,1,1,2,128,128]{5,4,3,2,1,0:T(8,128)}, u32[]{:S(2)}) copy-start(f32[3,1,1,2,128,128]{5,4,3,2,1,0:T(8,128)} %refs_2_.1) | copy-start | bytes 1179652
  2.4 0.9 %copy-start.1 = (f32[1,1,2,128,128]{4,3,2,1,0:T(8,128)S(1)}, f32[1,1,2,128,128]{4,3,2,1,0:T(8,128)}, u32[]{:S(2)}) copy-start(f32[1,1,2,128,128]{4,3,2,1,0:T(8,128)} %refs_1_.1) | copy-start | bytes 393220
  3.3 0.8 %copy-start.2 = (f32[1,1,2,32,128]{4,3,2,1,0:T(8,128)S(1)}, f32[1,1,2,32,128]{4,3,2,1,0:T(8,128)}, u32[]{:S(2)}) copy-start(f32[1,1,2,32,128]{4,3,2,1,0:T(8,128)} %refs_4_.1) | copy-start | bytes 98308

commit v2 on v1

--- a/solution.py
+++ b/solution.py
@@ -11,6 +11,7 @@
 ITERS = 3
 AXES = ("gx", "gy", "gz")
 COARSE_GROUPS = (("gy", "gz"), ("gx",))
+UNROLLED = 32
 DOT_GROUPS = (("gx", "gy", "gz"),)
 MESH = pl.DeviceIdType.MESH
 F32 = jnp.float32
@@ -44,7 +45,11 @@
         action(place(lax.rem(me + k, count), group, sizes))
         return carry
 
-    lax.fori_loop(1, count, body, 0)
+    if count <= UNROLLED:
+        for k in range(1, count):
+            body(k, 0)
+    else:
+        lax.fori_loop(1, count, body, 0)
 
 
 def split_rows(v):
@@ -85,7 +90,8 @@
 
 
 def kernel(sizes, lz, block, defl, *refs):
-    (right_ref, diag_ref, coup_ref, pat_ref, defl_ref, sol_ref, res_ref) = refs[:7]
+    inputs = refs[:5]
+    sol_ref, res_ref = refs[5:7]
     (loc_h, loc_l, out_h, out_l, in_h, in_l, zo_h, zo_l, zi_h, zi_l, proj_h, proj_l) = refs[7:19]
     n_ops = 1 + ITERS
     at = 19
@@ -97,7 +103,12 @@
     at += len(COARSE_GROUPS)
     dot_bufs = [refs[at + k * len(DOT_GROUPS) : at + (k + 1) * len(DOT_GROUPS)] for k in range(ITERS)]
     at += ITERS * len(DOT_GROUPS)
-    halo_send, halo_recv, red_send, red_recv = refs[at : at + 4]
+    halo_send, halo_recv, red_send, red_recv, load_sem = refs[at : at + 5]
+    staged = refs[at + 5 : at + 10]
+    loads = [pltpu.make_async_copy(src, dst, load_sem.at[k]) for k, (src, dst) in enumerate(zip(inputs, staged))]
+    for load in loads:
+        load.start()
+    right_ref, diag_ref, coup_ref, pat_ref, defl_ref = staged
 
     idx = {axis: lax.axis_index(axis) for axis in AXES}
     lower = {axis: idx[axis] > 0 for axis in AXES}
@@ -112,10 +123,13 @@
     def greet(peer):
         pl.semaphore_signal(barrier, inc=1, device_id=peer, device_id_type=MESH)
 
-    for_peers(AXES, sizes, greet)
+    for group in COARSE_GROUPS:
+        for_peers(group, sizes, greet)
+    for load in loads:
+        load.wait()
 
     def gate(d, c):
-        return pat_ref[d, 0, 0, c].astype(F32)
+        return pat_ref[0, 0, c : c + 1, d : d + 1].astype(F32)
 
     def put(ref_h, ref_l, rows, cols, value):
         high, low = split_pair(value)
@@ -179,18 +193,20 @@
         for sends, _, copy in copies:
             pl.when(sends)(copy.start)
 
-    def open_product(k, v):
+    def open_product(k, v, later=None):
         field, car_x, car_y, car_z = ops[k][:4]
-        copies = halo_copies(k)
+        copies = halo_copies(k) if later is None else None
         for c in range(lz):
             field[c] = v[:, span(c)]
-        start(copies[:3])
+        if later is None:
+            start(copies[:3])
         for c in range(lz):
             carried = times(v[:, span(c)], out_h[c], out_l[c])
             car_x[c] = carried[:, span(0)]
             car_y[c] = carried[:, span(1)]
         car_z[...] = times(v[:, span(lz - 1)], zo_h[...], zo_l[...])
-        start(copies[3:])
+        if later is None:
+            start(copies[3:])
         return times(v, loc_h[...], loc_l[...])
 
     def close_product(k, own):
@@ -239,7 +255,7 @@
 
     rows_first = ops[0][0].shape[1]
     first = jnp.concatenate([basis, right, jnp.zeros((rows_first - defl - 1, lz * block), F32)], axis=0)
-    pl.semaphore_wait(barrier, extent(AXES, sizes) - 1)
+    pl.semaphore_wait(barrier, sum(extent(group, sizes) - 1 for group in COARSE_GROUPS))
     own = open_product(0, first)
     proj_h[...] = jnp.zeros_like(proj_h)
     proj_l[...] = jnp.zeros_like(proj_l)
@@ -263,12 +279,13 @@
     sem = 0
     value = jnp.concatenate([packed, jnp.broadcast_to(right_local, (8, block))], axis=0)
     reduce_start(coarse_bufs[0], COARSE_GROUPS[0], sem, value)
-    own = open_product(1, applied)
+    own = open_product(1, applied, "later")
     put(proj_h, proj_l, slice(defl, block), everything, jnp.zeros((block - defl, lz * block), F32))
     for k in range(1, len(COARSE_GROUPS)):
         value = reduce_done(coarse_bufs[k - 1], sem)
         sem += 1
         reduce_start(coarse_bufs[k], COARSE_GROUPS[k], sem, value)
+    start(halo_copies(1))
     value = reduce_done(coarse_bufs[-1], sem)
     sem += 1
     coarse = jnp.concatenate(
@@ -348,6 +365,17 @@
         gathered(buf, red_send.at[k]).wait()
 
 
+def hand_out(sol_ref, res_ref, sol_out, res_out, sems):
+    copies = [
+        pltpu.make_async_copy(sol_ref, sol_out, sems.at[0]),
+        pltpu.make_async_copy(res_ref, res_out, sems.at[1]),
+    ]
+    for copy in copies:
+        copy.start()
+    for copy in copies:
+        copy.wait()
+
+
 def solution(mesh):
     sizes = dict(mesh.shape)
     in_specs = (
@@ -361,6 +389,7 @@
 
     def per_device(right_side, diag_blocks, couplings, pattern, deflation):
         lx, ly, lz, block = right_side.shape
+        pattern = jnp.transpose(pattern, (1, 2, 3, 0))
         assert lx == 1 and ly == 1
         defl = deflation.shape[3]
         rows_first = (defl + 1 + 7) // 8 * 8
@@ -388,19 +417,29 @@
         reductions = len(COARSE_GROUPS) + ITERS * len(DOT_GROUPS)
         scratch += [pltpu.SemaphoreType.DMA((1 + ITERS, 6))] * 2
         scratch += [pltpu.SemaphoreType.DMA((reductions,))] * 2
+        scratch.append(pltpu.SemaphoreType.DMA((5,)))
+        for array in (right_side, diag_blocks, couplings, pattern, deflation):
+            scratch.append(pltpu.VMEM(array.shape, array.dtype))
         vmem = pl.BlockSpec(memory_space=pltpu.VMEM)
-        smem = pl.BlockSpec(memory_space=pltpu.SMEM)
+        anywhere = pl.BlockSpec(memory_space=pl.ANY)
         out = jax.ShapeDtypeStruct(right_side.shape, F32)
-        return pl.pallas_call(
+        results = pl.pallas_call(
             functools.partial(kernel, sizes, lz, block, defl),
             out_shape=(out, out),
-            in_specs=[vmem, vmem, vmem, smem, vmem],
+            in_specs=[anywhere] * 5,
             out_specs=(vmem, vmem),
             scratch_shapes=scratch,
             compiler_params=pltpu.CompilerParams(
                 collective_id=0, has_side_effects=True, vmem_limit_bytes=48 * 1024 * 1024
             ),
         )(right_side, diag_blocks, couplings, pattern, deflation)
+        return pl.pallas_call(
+            hand_out,
+            out_shape=(out, out),
+            in_specs=[vmem, vmem],
+            out_specs=(anywhere, anywhere),
+            scratch_shapes=[pltpu.SemaphoreType.DMA((2,))],
+        )(*results)
 
     return jax.shard_map(
         per_device, mesh=mesh, in_specs=in_specs, out_specs=out_specs, check_vma=False

time: 41.9 us -> 42 us (level)
  local copies, waits for them, and re-layouts: 4.56 us -> 5.15 us
  Pallas kernels: 36.4 us -> 35.9 us
    pallas_call x1, Pallas kernels: 36.4 us -> 34.7 us  [per_device(): pl.pallas_call(functools.partial(kernel, sizes, lz, block, defl), out_sha...]
    pallas_call x0 -> x1, Pallas kernels: none -> 1.25 us  [per_device(): pl.pallas_call(hand_out, out_shape=(out, out), in_specs=[vmem, vmem], out...]
    unnamed x11 -> x14, local copies, waits for them, and re-layouts: 4.56 us -> 5.15 us
where the time goes in v2:
time: 42 us; the launch traced here: 41.8 us
  Pallas kernels  35.9 us (85%)
  local copies, waits for them, and re-layouts  5.15 us (12%)
  between operations  0.66 us (2%)
    pallas_call x1, Pallas kernels, per_device(): pl.pallas_call(functools.partial(kernel, sizes, lz, block, defl), out_sha...  34.7 us
    unnamed x14, local copies, waits for them, and re-layouts  5.15 us
    pallas_call x1, Pallas kernels, per_device(): pl.pallas_call(hand_out, out_shape=(out, out), in_specs=[vmem, vmem], out...  1.25 us

profile of v2, /device:TPU:0, one launch (start us, length us, event | category | flops | bytes accessed | tf_op | source)
XLA Modules:
  0.0 41.8 jit_solution(9473327483094960888)
XLA Ops:
  0.6 0.0 copy-start.3
  0.6 0.7 %copy-done.3 = f32[1,1,2,128]{3,2,1,0:T(2,128)S(1)} copy-done((f32[1,1,2,128]{3,2,1,0:T(2,128)S(1)}, f32[1,1,2,128]{3,2,1,0:T(2,128)}, u32[]{:S(2)}) %copy-start.3) | copy-done | bytes 1048
  1.3 0.0 copy-start
  1.3 1.0 %copy-done = f32[3,1,1,2,128,128]{5,4,3,2,1,0:T(8,128)S(1)} copy-done((f32[3,1,1,2,128,128]{5,4,3,2,1,0:T(8,128)S(1)}, f32[3,1,1,2,128,128]{5,4,3,2,1,0:T(8,128)}, u32[]{:S(2)}) %copy-start) | copy-done | bytes 393240
  2.3 0.0 copy-start.1
  2.3 0.9 %copy-done.1 = f32[1,1,2,128,128]{4,3,2,1,0:T(8,128)S(1)} copy-done((f32[1,1,2,128,128]{4,3,2,1,0:T(8,128)S(1)}, f32[1,1,2,128,128]{4,3,2,1,0:T(8,128)}, u32[]{:S(2)}) %copy-start.1) | copy-done | bytes 131096
  3.2 0.0 copy-start.2
  3.2 0.8 %copy-done.2 = f32[1,1,2,32,128]{4,3,2,1,0:T(8,128)S(1)} copy-done((f32[1,1,2,32,128]{4,3,2,1,0:T(8,128)S(1)}, f32[1,1,2,32,128]{4,3,2,1,0:T(8,128)}, u32[]{:S(2)}) %copy-start.2) | copy-done | bytes 32792
  4.0 0.0 copy-start.4
  4.0 0.7 %copy-done.4 = s32[3,1,1,2]{0,3,2,1:T(2,128)S(1)} copy-done((s32[3,1,1,2]{0,3,2,1:T(2,128)S(1)}, s32[3,1,1,2]{0,3,2,1:T(2,128)}, u32[]{:S(2)}) %copy-start.4) | copy-done | bytes 48
  4.7 34.7 %shard_map.68 = (f32[1,1,2,128]{3,2,1,0:T(2,128)S(1)}, f32[1,1,2,128]{3,2,1,0:T(2,128)S(1)}) custom-call(f32[1,1,2,128]{3,2,1,0:T(2,128)S(1)} %copy-done.3, f32[1,1,2,128,128]{4,3,2,1,0:T(8,128)S(1)} %copy-done.1, f32[3,1,1,2,128,128]{5,4,3,2,1,0:T(8,128)S(1)} %copy-done, s32[1,1,2,3]{3,2,1,0:T(2,128)S(1)} %bitcast.1, f32[1,1,2,32,128]{4,3,2,1,0:T(8,128)S(1)} %copy-done.2), custom_call_target="tpu_custom_call" | custom-call | tf_op jit(solution)/shard_map/pallas_call | solution.py:426
  39.4 0.0 copy-start.5
  39.4 0.6 %copy-done.5 = f32[1,1,2,128]{3,2,1,0:T(2,128)} copy-done((f32[1,1,2,128]{3,2,1,0:T(2,128)}, f32[1,1,2,128]{3,2,1,0:T(2,128)S(1)}, u32[]{:S(2)}) %copy-start.5) | copy-done | bytes 1048
  39.9 0.0 copy-start.6
  39.9 0.6 %copy-done.6 = f32[1,1,2,128]{3,2,1,0:T(2,128)} copy-done((f32[1,1,2,128]{3,2,1,0:T(2,128)}, f32[1,1,2,128]{3,2,1,0:T(2,128)S(1)}, u32[]{:S(2)}) %copy-start.6) | copy-done | bytes 1048
  40.5 1.3 %shard_map.69 = (f32[1,1,2,128]{3,2,1,0:T(2,128)}, f32[1,1,2,128]{3,2,1,0:T(2,128)}) custom-call(f32[1,1,2,128]{3,2,1,0:T(2,128)} %copy-done.5, f32[1,1,2,128]{3,2,1,0:T(2,128)} %copy-done.6), custom_call_target="tpu_custom_call" | custom-call | tf_op jit(solution)/shard_map/pallas_call | solution.py:436
Async XLA Ops:
  0.6 0.7 %copy-start.3 = (f32[1,1,2,128]{3,2,1,0:T(2,128)S(1)}, f32[1,1,2,128]{3,2,1,0:T(2,128)}, u32[]{:S(2)}) copy-start(f32[1,1,2,128]{3,2,1,0:T(2,128)} %refs_0_.1) | copy-start | bytes 3076
  1.3 1.0 %copy-start = (f32[3,1,1,2,128,128]{5,4,3,2,1,0:T(8,128)S(1)}, f32[3,1,1,2,128,128]{5,4,3,2,1,0:T(8,128)}, u32[]{:S(2)}) copy-start(f32[3,1,1,2,128,128]{5,4,3,2,1,0:T(8,128)} %refs_2_.1) | copy-start | bytes 1179652
  2.3 0.9 %copy-start.1 = (f32[1,1,2,128,128]{4,3,2,1,0:T(8,128)S(1)}, f32[1,1,2,128,128]{4,3,2,1,0:T(8,128)}, u32[]{:S(2)}) copy-start(f32[1,1,2,128,128]{4,3,2,1,0:T(8,128)} %refs_1_.1) | copy-start | bytes 393220
  3.2 0.8 %copy-start.2 = (f32[1,1,2,32,128]{4,3,2,1,0:T(8,128)S(1)}, f32[1,1,2,32,128]{4,3,2,1,0:T(8,128)}, u32[]{:S(2)}) copy-start(f32[1,1,2,32,128]{4,3,2,1,0:T(8,128)} %refs_4_.1) | copy-start | bytes 98308
  4.0 0.7 %copy-start.4 = (s32[3,1,1,2]{0,3,2,1:T(2,128)S(1)}, s32[3,1,1,2]{0,3,2,1:T(2,128)}, u32[]{:S(2)}) copy-start(s32[3,1,1,2]{0,3,2,1:T(2,128)} %param.8) | copy-start | bytes 76
  39.4 0.6 %copy-start.5 = (f32[1,1,2,128]{3,2,1,0:T(2,128)}, f32[1,1,2,128]{3,2,1,0:T(2,128)S(1)}, u32[]{:S(2)}) copy-start(f32[1,1,2,128]{3,2,1,0:T(2,128)S(1)} %get-tuple-element.4.sol_ref) | copy-start | bytes 3076
  39.9 0.6 %copy-start.6 = (f32[1,1,2,128]{3,2,1,0:T(2,128)}, f32[1,1,2,128]{3,2,1,0:T(2,128)S(1)}, u32[]{:S(2)}) copy-start(f32[1,1,2,128]{3,2,1,0:T(2,128)S(1)} %get-tuple-element.5.res_ref) | copy-start | bytes 3076

commit v3 on v2

--- a/solution.py
+++ b/solution.py
@@ -365,15 +365,16 @@
         gathered(buf, red_send.at[k]).wait()
 
 
-def hand_out(sol_ref, res_ref, sol_out, res_out, sems):
-    copies = [
-        pltpu.make_async_copy(sol_ref, sol_out, sems.at[0]),
-        pltpu.make_async_copy(res_ref, res_out, sems.at[1]),
-    ]
-    for copy in copies:
-        copy.start()
-    for copy in copies:
-        copy.wait()
+def hand_out(sol_ref, res_ref, sol_out, res_out, sol_held, res_held, sems):
+    def move(routes, k):
+        copies = [pltpu.make_async_copy(src, dst, sems.at[k, j]) for j, (src, dst) in enumerate(routes)]
+        for copy in copies:
+            copy.start()
+        for copy in copies:
+            copy.wait()
+
+    move(((sol_ref, sol_held), (res_ref, res_held)), 0)
+    move(((sol_held, sol_out), (res_held, res_out)), 1)
 
 
 def solution(mesh):
@@ -421,24 +422,26 @@
         for array in (right_side, diag_blocks, couplings, pattern, deflation):
             scratch.append(pltpu.VMEM(array.shape, array.dtype))
         vmem = pl.BlockSpec(memory_space=pltpu.VMEM)
+        hbm = pl.BlockSpec(memory_space=pltpu.HBM)
         anywhere = pl.BlockSpec(memory_space=pl.ANY)
         out = jax.ShapeDtypeStruct(right_side.shape, F32)
         results = pl.pallas_call(
             functools.partial(kernel, sizes, lz, block, defl),
             out_shape=(out, out),
-            in_specs=[anywhere] * 5,
+            in_specs=[hbm] * 5,
             out_specs=(vmem, vmem),
             scratch_shapes=scratch,
             compiler_params=pltpu.CompilerParams(
-                collective_id=0, has_side_effects=True, vmem_limit_bytes=48 * 1024 * 1024
+                collective_id=0, has_side_effects=True, vmem_limit_bytes=67_043_328
             ),
         )(right_side, diag_blocks, couplings, pattern, deflation)
         return pl.pallas_call(
             hand_out,
             out_shape=(out, out),
-            in_specs=[vmem, vmem],
-            out_specs=(anywhere, anywhere),
-            scratch_shapes=[pltpu.SemaphoreType.DMA((2,))],
+            in_specs=[anywhere, anywhere],
+            out_specs=(hbm, hbm),
+            scratch_shapes=[pltpu.VMEM(out.shape, F32)] * 2 + [pltpu.SemaphoreType.DMA((2, 2))],
+            compiler_params=pltpu.CompilerParams(vmem_limit_bytes=67_043_328),
         )(*results)
 
     return jax.shard_map(

time: 42 us -> 37 us (0.88)
  local copies, waits for them, and re-layouts: 5.15 us -> 0 us
    unnamed x14 -> x0, local copies, waits for them, and re-layouts: 5.15 us -> none
where the time goes in v3:
time: 37 us; the launch traced here: 36.8 us
  Pallas kernels  36.2 us (98%)
  between operations  0.64 us (2%)
    pallas_call x1, Pallas kernels, per_device(): pl.pallas_call(functools.partial(kernel, sizes, lz, block, defl), out_sha...  34.9 us
    pallas_call x1, Pallas kernels, per_device(): pl.pallas_call(hand_out, out_shape=(out, out), in_specs=[anywhere, anywhe...  1.26 us

profile of v3, /device:TPU:0, one launch (start us, length us, event | category | flops | bytes accessed | tf_op | source)
XLA Modules:
  0.0 36.8 jit_solution(507727702595340611)
XLA Ops:
  0.6 34.9 %shard_map.68 = (f32[1,1,2,128]{3,2,1,0:T(2,128)}, f32[1,1,2,128]{3,2,1,0:T(2,128)}) custom-call(f32[1,1,2,128]{3,2,1,0:T(2,128)} %refs_0_.1, f32[1,1,2,128,128]{4,3,2,1,0:T(8,128)} %refs_1_.1, f32[3,1,1,2,128,128]{5,4,3,2,1,0:T(8,128)} %refs_2_.1, s32[1,1,2,3]{3,2,1,0:T(2,128)} %bitcast.1, f32[1,1,2,32,128]{4,3,2,1,0:T(8,128)} %refs_4_.1), custom_call_target="tpu_custom_call" | custom-call | tf_op jit(solution)/shard_map/pallas_call | solution.py:428
  35.6 1.3 %shard_map.69 = (f32[1,1,2,128]{3,2,1,0:T(2,128)}, f32[1,1,2,128]{3,2,1,0:T(2,128)}) custom-call(f32[1,1,2,128]{3,2,1,0:T(2,128)} %get-tuple-element.4.sol_ref, f32[1,1,2,128]{3,2,1,0:T(2,128)} %get-tuple-element.5.res_ref), custom_call_target="tpu_custom_call" | custom-call | tf_op jit(solution)/shard_map/pallas_call | solution.py:438

commit v4 on v3

--- a/solution.py
+++ b/solution.py
@@ -101,8 +101,10 @@
         at += 9
     coarse_bufs = refs[at : at + len(COARSE_GROUPS)]
     at += len(COARSE_GROUPS)
-    dot_bufs = [refs[at + k * len(DOT_GROUPS) : at + (k + 1) * len(DOT_GROUPS)] for k in range(ITERS)]
-    at += ITERS * len(DOT_GROUPS)
+    moment_bufs = refs[at : at + len(COARSE_GROUPS)]
+    at += len(COARSE_GROUPS)
+    dot_bufs = [refs[at + k * len(DOT_GROUPS) : at + (k + 1) * len(DOT_GROUPS)] for k in range(ITERS - 1)]
+    at += (ITERS - 1) * len(DOT_GROUPS)
     halo_send, halo_recv, red_send, red_recv, load_sem = refs[at : at + 5]
     staged = refs[at + 5 : at + 10]
     loads = [pltpu.make_async_copy(src, dst, load_sem.at[k]) for k, (src, dst) in enumerate(zip(inputs, staged))]
@@ -272,64 +274,97 @@
         put(proj_h, proj_l, slice(g * defl, (g + 1) * defl), everything, applied)
     coarse_local = times_t(basis, proj_h[...], proj_l[...])
     lane = lax.broadcasted_iota(jnp.int32, (apart, block), 1)
-    packed = jnp.zeros((apart, block), F32)
-    for g in range(reps):
-        inside = (lane >= g * defl) & (lane < (g + 1) * defl)
-        packed = packed + jnp.where(inside, coarse_local[g * apart : (g + 1) * apart], 0.0)
-    sem = 0
-    value = jnp.concatenate([packed, jnp.broadcast_to(right_local, (8, block))], axis=0)
-    reduce_start(coarse_bufs[0], COARSE_GROUPS[0], sem, value)
-    own = open_product(1, applied, "later")
-    put(proj_h, proj_l, slice(defl, block), everything, jnp.zeros((block - defl, lz * block), F32))
-    for k in range(1, len(COARSE_GROUPS)):
-        value = reduce_done(coarse_bufs[k - 1], sem)
-        sem += 1
-        reduce_start(coarse_bufs[k], COARSE_GROUPS[k], sem, value)
-    start(halo_copies(1))
-    value = reduce_done(coarse_bufs[-1], sem)
-    sem += 1
-    coarse = jnp.concatenate(
-        [value[:apart]] + [pltpu.roll(value[:apart], block - g * defl, 1) for g in range(1, reps)], axis=0
-    )
+    lane_row = lax.broadcasted_iota(jnp.int32, (1, block), 1)
     col = lax.broadcasted_iota(jnp.int32, (defl, block), 1)
     row = lax.broadcasted_iota(jnp.int32, (defl, block), 0)
-    coarse = jnp.where(col < defl, coarse, 0.0)
+    eye = jnp.where(row == col, 1.0, 0.0)
+
+    def pack(repeated):
+        packed = jnp.zeros((apart, block), F32)
+        for g in range(reps):
+            inside = (lane >= g * defl) & (lane < (g + 1) * defl)
+            packed = packed + jnp.where(inside, repeated[g * apart : (g + 1) * apart], 0.0)
+        return packed
+
+    def unpack(packed):
+        groups = [packed] + [pltpu.roll(packed, block - g * defl, 1) for g in range(1, reps)]
+        return jnp.where(col < defl, jnp.concatenate(groups, axis=0), 0.0)
+
+    def on_applied(v):
+        return times_t(v, proj_h[...], proj_l[...])
+
+    stages = len(COARSE_GROUPS)
+    value = jnp.concatenate([pack(coarse_local), jnp.broadcast_to(right_local, (8, block))], axis=0)
+    reduce_start(coarse_bufs[0], COARSE_GROUPS[0], 0, value)
+    own = open_product(1, both)
+    second = pack(on_applied(applied))
+    h_right, h_image = on_applied(right), on_applied(image)
+    sq = jnp.sum(right * right, axis=1, keepdims=True)
+    cross = jnp.sum(right * image, axis=1, keepdims=True)
+    h_right = jnp.where(lane_row == defl, sq, jnp.where(lane_row == defl + 1, cross, h_right))
+    row8 = lax.broadcasted_iota(jnp.int32, (8, block), 0)
+    vectors = jnp.where(row8 == 0, h_right, h_image)
+    for k in range(1, stages):
+        value = reduce_done(coarse_bufs[k - 1], k - 1)
+        reduce_start(coarse_bufs[k], COARSE_GROUPS[k], k, value)
+    both_twice = close_product(1, own)
+    twice = both_twice[:defl]
+    image_twice = both_twice[defl : defl + 1]
+    moments = jnp.concatenate([second, pack(on_applied(twice)), vectors], axis=0)
+    reduce_start(moment_bufs[0], COARSE_GROUPS[0], stages, moments)
+    own = open_product(2, twice, "later")
+    value = reduce_done(coarse_bufs[-1], stages - 1)
+    coarse = unpack(value[:apart])
     square = jnp.concatenate([coarse, jnp.zeros((block - defl, block), F32)], axis=0)
     inv = 0.5 * (coarse + square.T[:defl])
     for k in range(defl):
+        if k == defl // 2:
+            for j in range(1, stages):
+                moments = reduce_done(moment_bufs[j - 1], stages + j - 1)
+                reduce_start(moment_bufs[j], COARSE_GROUPS[j], stages + j, moments)
+            start(halo_copies(2))
         pivot = 1.0 / inv[k : k + 1, k : k + 1]
         line = jnp.where(col[:1] == k, pivot, inv[k : k + 1] * pivot)
         inv = jnp.where(row == k, line, jnp.where(col == k, 0.0, inv) - inv[:, k : k + 1] * line)
-    eye = jnp.where(row == col, 1.0, 0.0)
 
     def coarse_solve(projected):
         return jnp.sum(inv * projected, axis=1, keepdims=True)
 
-    twice = close_product(1, own)
     coef = coarse_solve(value[apart : apart + 1])
+    coef_row = spread(coef, eye)
     x = spread(coef, basis)
     r = right - spread(coef, applied)
     w = image - spread(coef, twice)
+    moments = reduce_done(moment_bufs[-1], 2 * stages - 1)
+    h_right = moments[2 * apart : 2 * apart + 1]
+    h_image = moments[2 * apart + 1 : 2 * apart + 2]
+    onto = spread(coef, unpack(moments[:apart]))
+    onto_image = spread(coef, unpack(moments[apart : 2 * apart]))
+    sq = h_right[:, defl : defl + 1] + jnp.sum(coef_row * (onto - 2.0 * h_right), axis=1, keepdims=True)
+    cross = h_right[:, defl + 1 : defl + 2] + jnp.sum(coef_row * (onto_image - 2.0 * h_image), axis=1, keepdims=True)
+    total = jnp.where(lane_row == defl, sq, jnp.where(lane_row == defl + 1, cross, h_right - onto))
+    q = image_twice - spread(coef, close_product(2, own))
     d = s = z = curv = norm = None
-    lane_row = lax.broadcasted_iota(jnp.int32, (1, block), 1)
+    sem = 2 * stages
     for it in range(ITERS):
         last = it + 1 == ITERS
-        local = times_t(r, proj_h[...], proj_l[...])
-        sq = jnp.sum(r * r, axis=1, keepdims=True)
-        cross = jnp.sum(r * w, axis=1, keepdims=True)
-        local = jnp.where(lane_row == defl, sq, jnp.where(lane_row == defl + 1, cross, local))
-        bufs = dot_bufs[it]
-        reduce_start(bufs[0], DOT_GROUPS[0], sem, local)
-        if not last:
-            own = open_product(2 + it, w)
-        for k in range(1, len(DOT_GROUPS)):
-            local = reduce_done(bufs[k - 1], sem)
+        if it > 0:
+            local = on_applied(r)
+            sq = jnp.sum(r * r, axis=1, keepdims=True)
+            cross = jnp.sum(r * w, axis=1, keepdims=True)
+            local = jnp.where(lane_row == defl, sq, jnp.where(lane_row == defl + 1, cross, local))
+            bufs = dot_bufs[it - 1]
+            reduce_start(bufs[0], DOT_GROUPS[0], sem, local)
+            if not last:
+                own = open_product(2 + it, w)
+            for k in range(1, len(DOT_GROUPS)):
+                local = reduce_done(bufs[k - 1], sem)
+                sem += 1
+                reduce_start(bufs[k], DOT_GROUPS[k], sem, local)
+            if not last:
+                q = close_product(2 + it, own)
+            total = reduce_done(bufs[-1], sem)
             sem += 1
-            reduce_start(bufs[k], DOT_GROUPS[k], sem, local)
-        if not last:
-            q = close_product(2 + it, own)
-        total = reduce_done(bufs[-1], sem)
-        sem += 1
         coef = coarse_solve(total)
         mine = jnp.sum(eye * total, axis=1, keepdims=True)
         energy = jnp.sum(mine * coef, axis=0, keepdims=True)
@@ -360,7 +395,7 @@
     for k in range(n_ops):
         for sends, _, copy in halo_copies(k):
             pl.when(sends)(copy.wait_send)
-    every = list(coarse_bufs) + [buf for bufs in dot_bufs for buf in bufs]
+    every = list(coarse_bufs) + list(moment_bufs) + [buf for bufs in dot_bufs for buf in bufs]
     for k, buf in enumerate(every):
         gathered(buf, red_send.at[k]).wait()
 
@@ -405,17 +440,19 @@
             (block, wide),
         ):
             scratch += [pltpu.VMEM(shape, BF16)] * 2
-        for rows in (rows_first, defl) + (1,) * (ITERS - 1):
+        for rows in (rows_first, rows_first, defl) + (1,) * (ITERS - 2):
             layer, face = (lz, rows, block), (rows, block)
             scratch += [pltpu.VMEM(layer, F32)] * 3 + [pltpu.VMEM(face, F32)]
             scratch += [pltpu.VMEM(layer, F32)] * 2 + [pltpu.VMEM(face, F32)]
             scratch += [pltpu.VMEM((2,) + layer, F32), pltpu.VMEM(face, F32)]
         for group in COARSE_GROUPS:
             scratch.append(pltpu.VMEM((extent(group, sizes), defl * defl // block + 8, block), F32))
-        for _ in range(ITERS):
+        for group in COARSE_GROUPS:
+            scratch.append(pltpu.VMEM((extent(group, sizes), 2 * defl * defl // block + 8, block), F32))
+        for _ in range(ITERS - 1):
             for group in DOT_GROUPS:
                 scratch.append(pltpu.VMEM((extent(group, sizes), 1, block), F32))
-        reductions = len(COARSE_GROUPS) + ITERS * len(DOT_GROUPS)
+        reductions = 2 * len(COARSE_GROUPS) + (ITERS - 1) * len(DOT_GROUPS)
         scratch += [pltpu.SemaphoreType.DMA((1 + ITERS, 6))] * 2
         scratch += [pltpu.SemaphoreType.DMA((reductions,))] * 2
         scratch.append(pltpu.SemaphoreType.DMA((5,)))

time: 37 us -> 36.3 us (0.981)
  Pallas kernels: 36.2 us -> 35.5 us
    pallas_call x1, Pallas kernels: 34.9 us -> 34.2 us  [per_device(): pl.pallas_call(functools.partial(kernel, sizes, lz, block, defl), out_sha...]
where the time goes in v4:
time: 36.3 us; the launch traced here: 36.1 us
  Pallas kernels  35.5 us (98%)
  between operations  0.64 us (2%)
    pallas_call x1, Pallas kernels, per_device(): pl.pallas_call(functools.partial(kernel, sizes, lz, block, defl), out_sha...  34.2 us
    pallas_call x1, Pallas kernels, per_device(): pl.pallas_call(hand_out, out_shape=(out, out), in_specs=[anywhere, anywhe...  1.26 us

profile of v4, /device:TPU:0, one launch (start us, length us, event | category | flops | bytes accessed | tf_op | source)
XLA Modules:
  0.0 36.1 jit_solution(6307193496858170776)
XLA Ops:
  0.6 34.2 %shard_map.68 = (f32[1,1,2,128]{3,2,1,0:T(2,128)}, f32[1,1,2,128]{3,2,1,0:T(2,128)}) custom-call(f32[1,1,2,128]{3,2,1,0:T(2,128)} %refs_0_.1, f32[1,1,2,128,128]{4,3,2,1,0:T(8,128)} %refs_1_.1, f32[3,1,1,2,128,128]{5,4,3,2,1,0:T(8,128)} %refs_2_.1, s32[1,1,2,3]{3,2,1,0:T(2,128)} %bitcast.1, f32[1,1,2,32,128]{4,3,2,1,0:T(8,128)} %refs_4_.1), custom_call_target="tpu_custom_call" | custom-call | tf_op jit(solution)/shard_map/pallas_call | solution.py:465
  34.8 1.3 %shard_map.69 = (f32[1,1,2,128]{3,2,1,0:T(2,128)}, f32[1,1,2,128]{3,2,1,0:T(2,128)}) custom-call(f32[1,1,2,128]{3,2,1,0:T(2,128)} %get-tuple-element.4.sol_ref, f32[1,1,2,128]{3,2,1,0:T(2,128)} %get-tuple-element.5.res_ref), custom_call_target="tpu_custom_call" | custom-call | tf_op jit(solution)/shard_map/pallas_call | solution.py:475
